TPU v7x, 32 devices: a whole 2x2x4 slice. The times are simulated.
32 devices in a mesh: batch: 4 (over y, x), heads: 8 (over z, core).
Axes of the slice: x: 2, y: 2, z: 4, core: 2. Of those that a mesh axis runs over, the one named last changes fastest.
Arguments:
- draft_ids: int32 [192, 8], P('batch'), may hold values from 0 to 50279
- accepted: int32 [192], P('batch'), may hold values from 1 to 8
- embedding: bfloat16 [50280, 2560], P(None, 'heads'), may hold values from -6 to 6
- norm_gain: float32 [2, 2560], replicated, may hold values from 0.5 to 1.5
- w_zx: bfloat16 [2, 2560, 8, 128], P(None, None, 'heads'), may hold values from -0.125 to 0.125
- w_dt: bfloat16 [2, 2560, 8], P(None, None, 'heads'), may hold values from -0.125 to 0.125
- w_bc: bfloat16 [2, 2560, 256], P(None, None, 'heads'), may hold values from -0.125 to 0.125
- dt_bias: float32 [2, 8], P(None, 'heads'), may hold values from -4 to -1
- decay_rate: float32 [2, 8], P(None, 'heads'), may hold values from 1 to 16
- skip_weight: float32 [2, 8], P(None, 'heads'), may hold values from 0.5 to 1.5
- conv_x_w: bfloat16 [2, 4, 512], P(None, None, 'heads'), may hold values from -3 to 3
- conv_x_b: bfloat16 [2, 512], P(None, 'heads'), may hold values from -3 to 3
- conv_bc_w: bfloat16 [2, 4, 256], P(None, None, 'heads'), may hold values from -3 to 3
- conv_bc_b: bfloat16 [2, 256], P(None, 'heads'), may hold values from -3 to 3
- gate_gain: float32 [2, 512], P(None, 'heads'), may hold values from 0.5 to 1.5
- out_w: bfloat16 [2, 512, 2560], P(None, 'heads'), may hold values from -0.375 to 0.375
- ssm_state: float32 [2, 192, 8, 64, 128], P(None, 'batch', 'heads'), may hold values from -1.6 to 1.6
- conv_x_state: bfloat16 [2, 192, 3, 512], P(None, 'batch', None, 'heads'), may hold values from -6 to 6
- conv_bc_state: bfloat16 [2, 192, 3, 256], P(None, 'batch', None, 'heads'), may hold values from -6 to 6
Outputs:
- hidden_out: bfloat16 [1536, 2560], P('batch', 'heads')
- new_ssm: float32 [2, 192, 8, 64, 128], P(None, 'batch', 'heads')
- new_conv_x: bfloat16 [2, 192, 3, 512], P(None, 'batch', None, 'heads')
- new_conv_bc: bfloat16 [2, 192, 3, 256], P(None, 'batch', None, 'heads')
Inputs may be any that keep to these rules, and one draw needn't show every extreme that they name: `accepted`: the number of a sequence's draft tokens that are kept, counted from the first.
All inputs are finite; a program needn't handle non-finite values.
Results may differ from a plain program's by a relative error of at most 0.015.
Values may be sent and summed in bfloat16 or wider, within the bound.
A program may use at most 128 MiB of HBM per device.

v0:
```python
import jax
import jax.numpy as jnp
from jax import lax
from jax.sharding import PartitionSpec as P

LAYERS = 2
EPS = 1e-05


def rms_scale(total, count):
    return lax.rsqrt(total / count + EPS)


def convolve(window, weight, bias, count):
    weight = weight.astype(jnp.float32)
    acc = window[:, 0:count] * weight[0]
    for k in range(1, weight.shape[0]):
        acc = acc + window[:, k : k + count] * weight[k]
    return jax.nn.silu(acc + bias.astype(jnp.float32))


def keep_rows(window, accepted, kept_rows):
    last_start = window.shape[1] - kept_rows
    kept = window[:, 1 : 1 + kept_rows]
    for start in range(2, last_start + 1):
        kept = jnp.where(
            (accepted == start)[:, None, None], window[:, start : start + kept_rows], kept
        )
    return kept


def recur(decay, step, values, bmat, cmat, skip, state, accepted):
    kept = state
    outputs = []
    for t in range(values.shape[1]):
        state = (
            decay[:, t, None, None] * state
            + (step[:, t, None] * values[:, t])[:, :, None] * bmat[:, t, None, :]
        )
        outputs.append(jnp.sum(state * cmat[:, t, None, :], axis=-1) + skip * values[:, t])
        kept = jnp.where((accepted == t + 1)[:, None, None], state, kept)
    return (jnp.stack(outputs, 1), kept)


def spread_terms(u_rows, scale, weight):
    product = lax.dot_general(
        weight, u_rows, (((0,), (1,)), ((), ())), preferred_element_type=jnp.float32
    )
    return product * scale[None, :]


def token_scale(local_sq, inner):
    return rms_scale(lax.psum(local_sq, "heads"), inner)


def local(
    draft_ids,
    accepted,
    embedding,
    norm_gain,
    w_zx,
    w_dt,
    w_bc,
    dt_bias,
    decay_rate,
    skip_weight,
    conv_x_w,
    conv_x_b,
    conv_bc_w,
    conv_bc_b,
    gate_gain,
    out_w,
    ssm_state,
    conv_x_state,
    conv_bc_state,
):
    seq_rows, draft = draft_ids.shape
    heads_here = w_zx.shape[2]
    width = w_zx.shape[3] // 2
    local_inner = heads_here * width
    own_cols = embedding.shape[1]
    model = own_cols * lax.axis_size("heads")
    inner = local_inner * lax.axis_size("heads")
    bc_here = w_bc.shape[2]
    kernel = conv_x_w.shape[1]
    recur_heads = jax.vmap(recur, in_axes=(2, 2, 2, None, None, 0, 1, None), out_axes=(2, 1))
    whole_bc = (
        lax.all_gather(w_bc, "heads", axis=2, tiled=True),
        lax.all_gather(conv_bc_w, "heads", axis=2, tiled=True),
        lax.all_gather(conv_bc_b, "heads", axis=1, tiled=True),
        lax.all_gather(conv_bc_state, "heads", axis=3, tiled=True),
    )
    saved_state, saved_x, saved_bc = ([], [], [])

    def mixer(layer, stream):
        value = stream.astype(jnp.float32)
        normed = (
            value * rms_scale(jnp.sum(value * value, -1, keepdims=True), model) * norm_gain[layer]
        ).astype(jnp.bfloat16)
        zx = jnp.dot(
            normed, w_zx[layer].reshape(model, -1), preferred_element_type=jnp.float32
        ).astype(jnp.bfloat16)
        zx = zx.reshape(seq_rows, draft, heads_here, 2, width)
        gate_z = zx[:, :, :, 0].astype(jnp.float32)
        values = zx[:, :, :, 1].reshape(seq_rows, draft, local_inner)
        dt_raw = (
            jnp.dot(normed, w_dt[layer], preferred_element_type=jnp.float32)
            .astype(jnp.bfloat16)
            .reshape(seq_rows, draft, heads_here)
        )
        bc = (
            jnp.dot(normed, whole_bc[0][layer], preferred_element_type=jnp.float32)
            .astype(jnp.bfloat16)
            .reshape(seq_rows, draft, -1)
        )
        window_bc = jnp.concatenate([whole_bc[3][layer], bc], axis=1)
        bcc = convolve(
            window_bc.astype(jnp.float32), whole_bc[1][layer], whole_bc[2][layer], draft
        ).astype(jnp.bfloat16)
        kept_bc = keep_rows(window_bc, accepted, kernel - 1)
        bcc = lax.optimization_barrier(bcc).astype(jnp.float32)
        kept_bc = lax.dynamic_slice_in_dim(kept_bc, lax.axis_index("heads") * bc_here, bc_here, 2)
        states = bcc.shape[2] // 2
        bmat = bcc[..., :states]
        cmat = bcc[..., states:]
        window_x = jnp.concatenate([conv_x_state[layer], values], axis=1)
        xc = convolve(
            window_x.astype(jnp.float32), conv_x_w[layer], conv_x_b[layer], draft
        ).reshape(seq_rows, draft, heads_here, width)
        step = jax.nn.softplus(dt_raw.astype(jnp.float32) + dt_bias[layer])
        decay = jnp.exp(-step * decay_rate[layer])
        outputs, kept = recur_heads(
            decay, step, xc, bmat, cmat, skip_weight[layer], ssm_state[layer], accepted
        )
        saved_state.append(kept)
        saved_x.append(keep_rows(window_x, accepted, kernel - 1))
        saved_bc.append(kept_bc)
        gated = outputs * jax.nn.silu(gate_z)
        local_sq = jnp.sum(gated * gated, axis=(2, 3)).reshape(-1)
        u_rows = (
            (gated.reshape(seq_rows, draft, local_inner) * gate_gain[layer])
            .astype(jnp.bfloat16)
            .reshape(-1, local_inner)
        )
        return (u_rows, local_sq)

    part = embedding[draft_ids.reshape(-1)]
    stream = lax.all_gather(part, "heads", axis=1, tiled=True)
    where_cols = lax.axis_index("heads") * own_cols
    result = part
    for layer in range(LAYERS):
        u_rows, local_sq = mixer(layer, stream)
        scale = token_scale(local_sq, inner)
        if layer + 1 < LAYERS:
            term = (
                jnp.dot(u_rows, out_w[layer], preferred_element_type=jnp.float32) * scale[:, None]
            )
            total = lax.psum(term, "heads")
            stream = (stream.astype(jnp.float32) + total).astype(jnp.bfloat16)
        else:
            mine = lax.psum_scatter(
                spread_terms(u_rows, scale, out_w[layer]), "heads", scatter_dimension=0, tiled=True
            )
            own_stream = lax.dynamic_slice_in_dim(stream, where_cols, own_cols, 1)
            result = (own_stream.astype(jnp.float32) + mine.T).astype(jnp.bfloat16)
    return (result, jnp.stack(saved_state), jnp.stack(saved_x), jnp.stack(saved_bc))


def solution(mesh):
    placed = (
        P("batch", None),
        P("batch"),
        P(None, "heads"),
        P(),
        P(None, None, "heads", None),
        P(None, None, "heads"),
        P(None, None, "heads"),
        P(None, "heads"),
        P(None, "heads"),
        P(None, "heads"),
        P(None, None, "heads"),
        P(None, "heads"),
        P(None, None, "heads"),
        P(None, "heads"),
        P(None, "heads"),
        P(None, "heads", None),
        P(None, "batch", "heads", None, None),
        P(None, "batch", None, "heads"),
        P(None, "batch", None, "heads"),
    )
    return jax.shard_map(
        local,
        mesh=mesh,
        in_specs=placed,
        out_specs=(
            P("batch", "heads"),
            P(None, "batch", "heads", None, None),
            P(None, "batch", None, "heads"),
            P(None, "batch", None, "heads"),
        ),
        check_vma=False,
    )
```

profile of v0, /device:TPU:0, one launch (start us, length us, event | category | flops | bytes accessed | tf_op | source)
XLA Modules:
  0.0 371.8 jit_solution(4346947506731001234)
XLA Ops:
  7.2 43.7 %copy.113 = bf16[50280,320]{1,0:T(8,128)(2,1)} copy(bf16[50280,320]{0,1:T(8,128)(2,1)} %param.21) | data formatting | bytes 64358400 | tf_op args[2]
  51.2 7.8 %gather_fusion = bf16[384,320]{1,0:T(8,128)(2,1)S(1)} fusion(bf16[50280,320]{1,0:T(8,128)(2,1)} %copy.113, s32[1024]{0:T(1024)S(1)} %pad_clamp_fusion), kind=kCustom, calls=%fused_computation | custom fusion | bytes 493056 | tf_op jit(solution)/shard_map/gather | solution.py:147
  59.1 0.9 copy.114
  60.1 0.7 all-gather.5.cloned.1.call-update
  60.8 16.7 %all_gather.16 = bf16[2,48,3,256]{1,3,2,0:T(8,128)(2,1)S(1)} all-gather(bf16[2,48,3,32]{1,3,2,0:T(8,128)(2,1)S(1)} %copy-done.48), channel_id=1, replica_groups=mesh['batch'=4,'heads'=8] {'heads'}, dimensions={3}, use_global_device_ids=true | all-gather | bytes 165888 | tf_op jit(solution)/shard_map/all_gather | solution.py:91
  77.9 15.1 %all_gather.18 = bf16[2,4,256]{1,0,2:T(2,128)(2,1)S(1)} all-gather(bf16[2,4,32]{1,0,2:T(2,128)(2,1)S(1)} %copy.118), channel_id=1, replica_groups=mesh['batch'=4,'heads'=8] {'heads'}, dimensions={2}, use_global_device_ids=true | all-gather | bytes 4608 | tf_op jit(solution)/shard_map/all_gather | solution.py:89
  93.0 12.0 %all-gather.1 = bf16[8,32,2]{1,2,0:T(2,128)(2,1)S(1)} all-gather(bf16[1,32,2]{1,2,0:T(2,128)(2,1)S(1)} %bitcast.580), channel_id=1, replica_groups=mesh['batch'=4,'heads'=8] {'heads'}, dimensions={0}, use_global_device_ids=true | all-gather | bytes 1152 | tf_op jit(solution)/shard_map/all_gather | solution.py:90
  107.1 2.9 slice_reduce_fusion.7
  111.3 2.7 copy.115
  114.5 0.8 copy-done.83
  115.3 0.7 convolution_convert_fusion.1
  116.6 0.7 convolution_reduce_fusion.1
  118.0 0.7 multiply_exponential_fusion.1
  119.7 7.5 %all-gather.5.cloned.1.call-done = bf16[2,2560,256]{1,2,0:T(8,128)(2,1)} async-done(((bf16[2,2560,32]{1,2,0:T(8,128)(2,1)}), bf16[2,2560,256]{1,2,0:T(8,128)(2,1)}) %all-gather.5.cloned.1.call-update) | async-done | bytes 2621456 | tf_op jit(solution)/shard_map/all_gather | solution.py:88
  127.2 2.0 fusion.15
  130.1 1.1 copy-done
  131.2 4.1 %multiply_add_fusion.8 = (f32[1,48,64,128]{3,2,1,0:T(8,128)S(1)}, f32[1,48,64,128]{3,2,1,0:T(8,128)S(1)}, f32[48,64]{1,0:T(8,128)S(1)}, f32[48,64]{1,0:T(8,128)S(1)}) fusion(f32[48,128]{1,0:T(8,128)S(1)} %bitcast.537, f32[48,64]{1,0:T(8,128)S(1)} %get-tuple-element.186, f32[48]{0:T(128)S(1)} %get-tuple-element.237, f32[48,128]{1,0:T(8,128)S(1)} %bitcast.525, ...), kind=kLoop, calls=%fused_computation.43 | loop fusion | flops 7464960 | bytes 4977600 | tf_op jit(solution)/shard_map/vmap()/add | solution.py:37
  136.0 1.6 multiply_reduce_fusion.12
  139.5 3.7 multiply_reduce_fusion.8
  145.9 15.0 %psum.21 = f32[384]{0:T(512)S(1)} all-reduce(f32[384]{0:T(512)S(1)} %reshape.2511), channel_id=1, replica_groups=mesh['batch'=4,'heads'=8] {'heads'}, use_global_device_ids=true, to_apply=%region_10.11 | all-reduce | flops 384 | bytes 3072 | tf_op jit(solution)/shard_map/psum | solution.py:53
  160.9 3.5 convolution_multiply_fusion.1
  164.8 0.8 copy.125
  165.6 2.9 slice_reduce_fusion.3
  168.5 85.9 %all-reduce.2.cloned.1.call-done = f32[384,2560]{1,0:T(8,128)} async-done(((f32[384,2560]{1,0:T(8,128)}), f32[384,2560]{1,0:T(8,128)}) %all-reduce.2.cloned.1.call-update) | async-done | bytes 3932176 | tf_op jit(solution)/shard_map/psum | solution.py:158
  254.3 2.9 fusion.1
  257.3 0.7 convolution_convert_fusion
  258.5 0.7 convolution_reduce_fusion
  259.4 1.0 fusion.121
  261.1 0.8 fusion.128
  261.9 0.8 fusion.129
  264.7 2.1 fusion.14
  267.6 1.0 bitcast_multiply_fusion.2
  268.8 4.1 %multiply_add_fusion.2 = (f32[1,48,64,128]{3,2,1,0:T(8,128)S(1)}, f32[1,48,64,128]{3,2,1,0:T(8,128)S(1)}, f32[48,64]{1,0:T(8,128)S(1)}, f32[48,64]{1,0:T(8,128)S(1)}) fusion(f32[48,128]{1,0:T(8,128)S(1)} %bitcast.551, f32[48,64]{1,0:T(8,128)S(1)} %get-tuple-element.160, f32[48]{0:T(128)S(1)} %get-tuple-element.51, f32[48,128]{1,0:T(8,128)S(1)} %bitcast.528, ...), kind=kLoop, calls=%fused_computation.29 | loop fusion | flops 7464960 | bytes 4977600 | tf_op jit(solution)/shard_map/vmap()/add | solution.py:37
  273.0 1.2 constant_dynamic-update-slice_fusion.23
  274.2 1.6 multiply_reduce_fusion.4
  275.9 1.2 constant_dynamic-update-slice_fusion.22
  277.1 1.2 constant_dynamic-update-slice_fusion.21
  278.3 1.2 constant_dynamic-update-slice_fusion.20
  279.5 3.7 multiply_reduce_fusion
  283.2 1.2 constant_dynamic-update-slice_fusion.19
  284.4 1.2 constant_dynamic-update-slice_fusion.18
  285.6 1.2 constant_dynamic-update-slice_fusion.17
  286.7 1.9 constant_dynamic-update-slice_fusion.16
  288.8 0.7 copy.135
  289.5 0.8 reshape.2516
  290.3 15.7 %psum.23 = f32[384]{0:T(512)S(1)} all-reduce(f32[384]{0:T(512)S(1)} %reshape.2516), channel_id=1, replica_groups=mesh['batch'=4,'heads'=8] {'heads'}, use_global_device_ids=true, to_apply=%region_22.23 | all-reduce | flops 384 | bytes 3072 | tf_op jit(solution)/shard_map/psum | solution.py:53
  306.0 1.1 fusion.71
  307.1 3.5 fusion
  310.6 5.6 %copy.139 = f32[2560,384]{1,0:T(8,128)} copy(f32[2560,384]{0,1:T(8,128)} %fusion) | data formatting | bytes 7864320
  316.2 1.2 broadcast_compare_fusion.7
  317.5 1.7 fusion.105
  319.1 1.4 fusion.119
  320.6 0.7 dynamic-slice_select_fusion.6
  321.3 0.7 copy.136
  322.0 9.0 %select_select_fusion.1 = f32[1,48,1,64,128]{4,3,2,1,0:T(8,128)} fusion(f32[2,48,1,64,128]{4,3,2,1,0:T(8,128)S(1)} %copy-done.1, f32[48,128]{1,0:T(8,128)} %bitcast.536, f32[48,64]{1,0:T(8,128)} %copy-done.34, f32[48,128]{1,0:T(8,128)} %bitcast.534, f32[48,64]{1,0:T(8,128)} %copy-done.35, f32[48,128]{1,0:T(8,128)} %bitcast.532, f32[48,64]{1,0:T(8,128)} %copy-done.33, ...), kind=kLoop, calls=%fused_computation.22 | loop fusion | flops 12582912 | bytes 3442560 | tf_op jit(solution)/shard_map/vmap(jit(_where))/select_n | solution.py:41
  332.4 1.4 pad_maximum_fusion.6
  333.8 0.9 fusion.106
  334.7 1.4 pad_maximum_fusion.5
  336.1 8.2 %select_select_fusion = f32[1,48,1,64,128]{4,3,2,1,0:T(8,128)S(1)} fusion(f32[2,48,1,64,128]{4,3,2,1,0:T(8,128)S(1)} %copy-done.1, f32[48,128]{1,0:T(8,128)} %bitcast.550, f32[48,64]{1,0:T(8,128)} %copy-done.40, f32[48,128]{1,0:T(8,128)} %bitcast.548, f32[48,64]{1,0:T(8,128)} %copy-done.42, f32[48,128]{1,0:T(8,128)} %bitcast.546, f32[48,64]{1,0:T(8,128)} %copy-done.41, ...), kind=kLoop, calls=%fused_computation.21 | loop fusion | flops 12582912 | bytes 3442560 | tf_op jit(solution)/shard_map/vmap(jit(_where))/select_n | solution.py:41
  344.4 1.9 pad_maximum_fusion
  346.3 15.7 %reduce-scatter.4.cloned.1.call-done = f32[320,384]{1,0:T(8,128)} async-done(((f32[2560,384]{1,0:T(8,128)}), f32[320,384]{1,0:T(8,128)}) %reduce-scatter.4.cloned.1.call-update) | async-done | bytes 491536
  361.9 1.3 copy.140
  363.2 1.2 fusion.20
  364.4 0.9 copy.138
  (243 shorter events, 18.1 us)
Async XLA Ops:
  7.2 43.8 %copy-start.73 = (s32[48,8]{0,1:T(8,128)S(1)}, s32[48,8]{0,1:T(8,128)}, u32[]{:S(2)}) copy-start(s32[48,8]{0,1:T(8,128)} %param.19) | copy-start | bytes 4612
  7.2 104.1 %all-gather.7.cloned.1.call-start = ((), (), s32[]{:S(2)}) async-start(), calls=%async_computation.3 | async-start | bytes 2211840 | tf_op jit(solution)/shard_map/all_gather | solution.py:148
  51.2 9.7 %copy-start.48 = (bf16[2,48,3,32]{1,3,2,0:T(8,128)(2,1)S(1)}, bf16[2,48,3,32]{1,3,2,0:T(8,128)(2,1)}, u32[]{:S(2)}) copy-start(bf16[2,48,3,32]{1,3,2,0:T(8,128)(2,1)} %param.37) | copy-start | bytes 55300
  59.0 18.7 %copy-start.75 = (bf16[2,4,32]{2,1,0:T(4,128)(2,1)S(1)}, bf16[2,4,32]{2,1,0:T(4,128)(2,1)}, u32[]{:S(2)}) copy-start(bf16[2,4,32]{2,1,0:T(4,128)(2,1)} %param.31) | copy-start | bytes 1540
  59.0 34.0 %copy-start.82 = (bf16[2,32]{1,0:T(2,128)(2,1)S(1)}, bf16[2,32]{1,0:T(2,128)(2,1)}, u32[]{:S(2)}) copy-start(bf16[2,32]{1,0:T(2,128)(2,1)} %param.32) | copy-start | bytes 388
  59.0 46.1 %copy-start.77 = (f32[2,1]{0,1:T(1,128)S(1)}, f32[2,1]{0,1:T(1,128)}, u32[]{:S(2)}) copy-start(f32[2,1]{0,1:T(1,128)} %param.26) | copy-start | bytes 28
  59.0 46.7 %copy-start.78 = (f32[2,1]{0,1:T(1,128)S(1)}, f32[2,1]{0,1:T(1,128)}, u32[]{:S(2)}) copy-start(f32[2,1]{0,1:T(1,128)} %param.27) | copy-start | bytes 28
  59.1 47.3 %copy-start.79 = (f32[2,1]{0,1:T(1,128)S(1)}, f32[2,1]{0,1:T(1,128)}, u32[]{:S(2)}) copy-start(f32[2,1]{0,1:T(1,128)} %param.28) | copy-start | bytes 28
  59.1 47.8 %copy-start.55 = (f32[2,2560]{1,0:T(2,128)S(1)}, f32[2,2560]{1,0:T(2,128)}, u32[]{:S(2)}) copy-start(f32[2,2560]{1,0:T(2,128)} %param.22) | copy-start | bytes 61444
  60.0 50.1 %copy-start.80 = (bf16[2,64]{1,0:T(2,128)(2,1)S(1)}, bf16[2,64]{1,0:T(2,128)(2,1)}, u32[]{:S(2)}) copy-start(bf16[2,64]{1,0:T(2,128)(2,1)} %param.30) | copy-start | bytes 772
  60.0 50.1 %copy-start.81 = (f32[2,64]{1,0:T(2,128)S(1)}, f32[2,64]{1,0:T(2,128)}, u32[]{:S(2)}) copy-start(f32[2,64]{1,0:T(2,128)} %param.33) | copy-start | bytes 1540
  60.0 51.2 %copy-start.76 = (bf16[2,4,64]{2,1,0:T(4,128)(2,1)S(1)}, bf16[2,4,64]{2,1,0:T(4,128)(2,1)}, u32[]{:S(2)}) copy-start(bf16[2,4,64]{2,1,0:T(4,128)(2,1)} %param.29) | copy-start | bytes 3076
  60.0 51.2 %copy-start.47 = (bf16[2,48,3,64]{3,1,2,0:T(8,128)(2,1)S(1)}, bf16[2,48,3,64]{3,1,2,0:T(8,128)(2,1)}, u32[]{:S(2)}) copy-start(bf16[2,48,3,64]{3,1,2,0:T(8,128)(2,1)} %param.36) | copy-start | bytes 110596
  60.0 67.2 %all-gather.5.cloned.1.call-start = ((), (), s32[]{:S(2)}) async-start(), calls=%async_computation.1 | async-start | bytes 2949120 | tf_op jit(solution)/shard_map/all_gather | solution.py:88
  60.8 193.6 %all-reduce.2.cloned.1.call-start = ((), (), s32[]{:S(2)}) async-start(), calls=%async_computation.2 | async-start | bytes 7864320 | tf_op jit(solution)/shard_map/psum | solution.py:158
  77.8 51.5 %copy-start.10 = (bf16[48,3,256]{2,1,0:T(4,128)(2,1)}, bf16[48,3,256]{2,1,0:T(4,128)(2,1)S(1)}, u32[]{:S(2)}) copy-start(bf16[48,3,256]{2,1,0:T(4,128)(2,1)S(1)} %copy.117) | copy-start | bytes 221188
  111.2 8.1 %copy-start.18 = (bf16[48,3,64]{2,0,1:T(8,128)(2,1)}, bf16[48,3,64]{2,0,1:T(8,128)(2,1)S(1)}, u32[]{:S(2)}) copy-start(bf16[48,3,64]{2,0,1:T(8,128)(2,1)S(1)} %get-tuple-element.194) | copy-start | bytes 55300
  111.3 149.2 %copy-start.17 = (bf16[48,3,64]{2,0,1:T(8,128)(2,1)}, bf16[48,3,64]{2,0,1:T(8,128)(2,1)S(1)}, u32[]{:S(2)}) copy-start(bf16[48,3,64]{2,0,1:T(8,128)(2,1)S(1)} %get-tuple-element.193) | copy-start | bytes 55300
  119.2 10.8 %copy-start.58 = (f32[48]{0:T(128)}, f32[48]{0:T(128)S(1)}, u32[]{:S(2)}) copy-start(f32[48]{0:T(128)S(1)} %get-tuple-element.233) | copy-start | bytes 580
  119.2 10.8 %copy-start.59 = (f32[48]{0:T(128)}, f32[48]{0:T(128)S(1)}, u32[]{:S(2)}) copy-start(f32[48]{0:T(128)S(1)} %get-tuple-element.234) | copy-start | bytes 580
  119.2 10.8 %copy-start.60 = (f32[48]{0:T(128)}, f32[48]{0:T(128)S(1)}, u32[]{:S(2)}) copy-start(f32[48]{0:T(128)S(1)} %get-tuple-element.235) | copy-start | bytes 580
  119.3 10.8 %copy-start.61 = (f32[48]{0:T(128)}, f32[48]{0:T(128)S(1)}, u32[]{:S(2)}) copy-start(f32[48]{0:T(128)S(1)} %get-tuple-element.237) | copy-start | bytes 580
  119.3 16.7 %copy-start.56 = (f32[48]{0:T(128)}, f32[48]{0:T(128)S(1)}, u32[]{:S(2)}) copy-start(f32[48]{0:T(128)S(1)} %get-tuple-element.236) | copy-start | bytes 580
  119.3 20.1 %copy-start.66 = (f32[48]{0:T(128)}, f32[48]{0:T(128)S(1)}, u32[]{:S(2)}) copy-start(f32[48]{0:T(128)S(1)} %get-tuple-element.238) | copy-start | bytes 580
  119.3 20.1 %copy-start.67 = (f32[48]{0:T(128)}, f32[48]{0:T(128)S(1)}, u32[]{:S(2)}) copy-start(f32[48]{0:T(128)S(1)} %get-tuple-element.239) | copy-start | bytes 580
  119.3 20.1 %copy-start.68 = (f32[48]{0:T(128)}, f32[48]{0:T(128)S(1)}, u32[]{:S(2)}) copy-start(f32[48]{0:T(128)S(1)} %get-tuple-element.240) | copy-start | bytes 580
  119.6 10.5 %copy-start.36 = (f32[48,64]{1,0:T(8,128)}, f32[48,64]{1,0:T(8,128)S(1)}, u32[]{:S(2)}) copy-start(f32[48,64]{1,0:T(8,128)S(1)} %get-tuple-element.186) | copy-start | bytes 36868
  119.6 10.5 %copy-start.37 = (f32[48,64]{1,0:T(8,128)}, f32[48,64]{1,0:T(8,128)S(1)}, u32[]{:S(2)}) copy-start(f32[48,64]{1,0:T(8,128)S(1)} %get-tuple-element.188) | copy-start | bytes 36868
  119.6 10.5 %copy-start.38 = (f32[48,64]{1,0:T(8,128)}, f32[48,64]{1,0:T(8,128)S(1)}, u32[]{:S(2)}) copy-start(f32[48,64]{1,0:T(8,128)S(1)} %get-tuple-element.189) | copy-start | bytes 36868
  119.6 10.5 %copy-start.39 = (f32[48,64]{1,0:T(8,128)}, f32[48,64]{1,0:T(8,128)S(1)}, u32[]{:S(2)}) copy-start(f32[48,64]{1,0:T(8,128)S(1)} %get-tuple-element.190) | copy-start | bytes 36868
  119.6 16.3 %copy-start.15 = (f32[48,64]{1,0:T(8,128)}, f32[48,64]{1,0:T(8,128)S(1)}, u32[]{:S(2)}) copy-start(f32[48,64]{1,0:T(8,128)S(1)} %get-tuple-element.187) | copy-start | bytes 36868
  119.7 19.8 %copy-start.33 = (f32[48,64]{1,0:T(8,128)}, f32[48,64]{1,0:T(8,128)S(1)}, u32[]{:S(2)}) copy-start(f32[48,64]{1,0:T(8,128)S(1)} %get-tuple-element.183) | copy-start | bytes 36868
  119.7 19.8 %copy-start.34 = (f32[48,64]{1,0:T(8,128)}, f32[48,64]{1,0:T(8,128)S(1)}, u32[]{:S(2)}) copy-start(f32[48,64]{1,0:T(8,128)S(1)} %get-tuple-element.184) | copy-start | bytes 36868
  119.7 19.8 %copy-start.35 = (f32[48,64]{1,0:T(8,128)}, f32[48,64]{1,0:T(8,128)S(1)}, u32[]{:S(2)}) copy-start(f32[48,64]{1,0:T(8,128)S(1)} %get-tuple-element.185) | copy-start | bytes 36868
  130.0 5.4 %copy-start.22 = (f32[48,1,128]{2,1,0:T(1,128)}, f32[48,1,128]{2,1,0:T(1,128)S(1)}, u32[]{:S(2)}) copy-start(f32[48,1,128]{2,1,0:T(1,128)S(1)} %get-tuple-element.174) | copy-start | bytes 73732
  130.0 5.4 %copy-start.23 = (f32[48,1,128]{2,1,0:T(1,128)}, f32[48,1,128]{2,1,0:T(1,128)S(1)}, u32[]{:S(2)}) copy-start(f32[48,1,128]{2,1,0:T(1,128)S(1)} %get-tuple-element.178) | copy-start | bytes 73732
  130.0 5.4 %copy-start.24 = (f32[48,1,128]{2,1,0:T(1,128)}, f32[48,1,128]{2,1,0:T(1,128)S(1)}, u32[]{:S(2)}) copy-start(f32[48,1,128]{2,1,0:T(1,128)S(1)} %get-tuple-element.180) | copy-start | bytes 73732
  130.0 5.4 %copy-start.25 = (f32[48,1,128]{2,1,0:T(1,128)}, f32[48,1,128]{2,1,0:T(1,128)S(1)}, u32[]{:S(2)}) copy-start(f32[48,1,128]{2,1,0:T(1,128)S(1)} %get-tuple-element.181) | copy-start | bytes 73732
  130.0 6.0 %copy-start.13 = (f32[48,1,128]{2,1,0:T(1,128)}, f32[48,1,128]{2,1,0:T(1,128)S(1)}, u32[]{:S(2)}) copy-start(f32[48,1,128]{2,1,0:T(1,128)S(1)} %get-tuple-element.176) | copy-start | bytes 73732
  130.0 9.5 %copy-start.19 = (f32[48,1,128]{2,1,0:T(1,128)}, f32[48,1,128]{2,1,0:T(1,128)S(1)}, u32[]{:S(2)}) copy-start(f32[48,1,128]{2,1,0:T(1,128)S(1)} %get-tuple-element.170) | copy-start | bytes 73732
  130.0 9.5 %copy-start.20 = (f32[48,1,128]{2,1,0:T(1,128)}, f32[48,1,128]{2,1,0:T(1,128)S(1)}, u32[]{:S(2)}) copy-start(f32[48,1,128]{2,1,0:T(1,128)S(1)} %get-tuple-element.171) | copy-start | bytes 73732
  130.0 9.5 %copy-start.21 = (f32[48,1,128]{2,1,0:T(1,128)}, f32[48,1,128]{2,1,0:T(1,128)S(1)}, u32[]{:S(2)}) copy-start(f32[48,1,128]{2,1,0:T(1,128)S(1)} %get-tuple-element.172) | copy-start | bytes 73732
  164.5 197.4 %reduce-scatter.4.cloned.1.call-start = ((), (), s32[]{:S(2)}) async-start(), calls=%async_computation.4 | async-start | bytes 4423680
  264.6 9.6 %copy-start.57 = (f32[48]{0:T(128)}, f32[48]{0:T(128)S(1)}, u32[]{:S(2)}) copy-start(f32[48]{0:T(128)S(1)} %get-tuple-element.52) | copy-start | bytes 580
  264.6 14.8 %copy-start.69 = (f32[48]{0:T(128)}, f32[48]{0:T(128)S(1)}, u32[]{:S(2)}) copy-start(f32[48]{0:T(128)S(1)} %get-tuple-element.48) | copy-start | bytes 580
  264.6 14.8 %copy-start.70 = (f32[48]{0:T(128)}, f32[48]{0:T(128)S(1)}, u32[]{:S(2)}) copy-start(f32[48]{0:T(128)S(1)} %get-tuple-element.49) | copy-start | bytes 580
  264.7 14.8 %copy-start.71 = (f32[48]{0:T(128)}, f32[48]{0:T(128)S(1)}, u32[]{:S(2)}) copy-start(f32[48]{0:T(128)S(1)} %get-tuple-element.50) | copy-start | bytes 580
  267.5 5.5 %copy-start.29 = (f32[48,1,128]{2,1,0:T(1,128)}, f32[48,1,128]{2,1,0:T(1,128)S(1)}, u32[]{:S(2)}) copy-start(f32[48,1,128]{2,1,0:T(1,128)S(1)} %get-tuple-element.149) | copy-start | bytes 73732
  267.5 5.5 %copy-start.30 = (f32[48,1,128]{2,1,0:T(1,128)}, f32[48,1,128]{2,1,0:T(1,128)S(1)}, u32[]{:S(2)}) copy-start(f32[48,1,128]{2,1,0:T(1,128)S(1)} %get-tuple-element.153) | copy-start | bytes 73732
  267.5 5.5 %copy-start.31 = (f32[48,1,128]{2,1,0:T(1,128)}, f32[48,1,128]{2,1,0:T(1,128)S(1)}, u32[]{:S(2)}) copy-start(f32[48,1,128]{2,1,0:T(1,128)S(1)} %get-tuple-element.155) | copy-start | bytes 73732
  267.5 5.5 %copy-start.32 = (f32[48,1,128]{2,1,0:T(1,128)}, f32[48,1,128]{2,1,0:T(1,128)S(1)}, u32[]{:S(2)}) copy-start(f32[48,1,128]{2,1,0:T(1,128)S(1)} %get-tuple-element.156) | copy-start | bytes 73732
  267.5 6.7 %copy-start.14 = (f32[48,1,128]{2,1,0:T(1,128)}, f32[48,1,128]{2,1,0:T(1,128)S(1)}, u32[]{:S(2)}) copy-start(f32[48,1,128]{2,1,0:T(1,128)S(1)} %get-tuple-element.151) | copy-start | bytes 73732
  267.5 11.9 %copy-start.26 = (f32[48,1,128]{2,1,0:T(1,128)}, f32[48,1,128]{2,1,0:T(1,128)S(1)}, u32[]{:S(2)}) copy-start(f32[48,1,128]{2,1,0:T(1,128)S(1)} %get-tuple-element.145) | copy-start | bytes 73732
  267.5 11.9 %copy-start.27 = (f32[48,1,128]{2,1,0:T(1,128)}, f32[48,1,128]{2,1,0:T(1,128)S(1)}, u32[]{:S(2)}) copy-start(f32[48,1,128]{2,1,0:T(1,128)S(1)} %get-tuple-element.146) | copy-start | bytes 73732
  267.6 11.9 %copy-start.28 = (f32[48,1,128]{2,1,0:T(1,128)}, f32[48,1,128]{2,1,0:T(1,128)S(1)}, u32[]{:S(2)}) copy-start(f32[48,1,128]{2,1,0:T(1,128)S(1)} %get-tuple-element.147) | copy-start | bytes 73732
  268.6 10.9 %copy-start.40 = (f32[48,64]{1,0:T(8,128)}, f32[48,64]{1,0:T(8,128)S(1)}, u32[]{:S(2)}) copy-start(f32[48,64]{1,0:T(8,128)S(1)} %bitcast_multiply_fusion.2) | copy-start | bytes 36868
  268.7 5.5 %copy-start.16 = (f32[48,64]{1,0:T(8,128)}, f32[48,64]{1,0:T(8,128)S(1)}, u32[]{:S(2)}) copy-start(f32[48,64]{1,0:T(8,128)S(1)} %get-tuple-element.161) | copy-start | bytes 36868
  268.7 10.7 %copy-start.41 = (f32[48,64]{1,0:T(8,128)}, f32[48,64]{1,0:T(8,128)S(1)}, u32[]{:S(2)}) copy-start(f32[48,64]{1,0:T(8,128)S(1)} %get-tuple-element.158) | copy-start | bytes 36868
  268.8 10.7 %copy-start.42 = (f32[48,64]{1,0:T(8,128)}, f32[48,64]{1,0:T(8,128)S(1)}, u32[]{:S(2)}) copy-start(f32[48,64]{1,0:T(8,128)S(1)} %get-tuple-element.159) | copy-start | bytes 36868
  275.9 12.8 %copy-start.8 = (bf16[48,8,1,1,64]{4,3,1,0,2:T(2,128)(2,1)S(1)}, bf16[48,8,1,1,64]{4,3,1,0,2:T(2,128)(2,1)}, u32[]{:S(2)}) copy-start(bf16[48,8,1,1,64]{4,3,1,0,2:T(2,128)(2,1)} %get-tuple-element.140) | copy-start | bytes 147460
  275.9 30.1 %copy-start.74 = (f32[64]{0:T(128)S(1)}, f32[64]{0:T(128)}, u32[]{:S(2)}) copy-start(f32[64]{0:T(128)} %get-tuple-element.209) | copy-start | bytes 772
  322.0 9.0 %copy-start.12 = (bf16[48,3,256]{2,1,0:T(4,128)(2,1)S(1)}, bf16[48,3,256]{2,1,0:T(4,128)(2,1)}, u32[]{:S(2)}) copy-start(bf16[48,3,256]{2,1,0:T(4,128)(2,1)} %copy.125) | copy-start | bytes 221188
  322.0 9.0 %copy-start.54 = (pred[48]{0:T(512)(128)(4,1)S(1)}, pred[48]{0:T(512)(128)(4,1)}, u32[]{:S(2)}) copy-start(pred[48]{0:T(512)(128)(4,1)} %copy-done.53) | copy-start | bytes 148
  336.1 8.3 %copy-start.2 = (f32[1,48,1,64,128]{4,3,2,1,0:T(8,128)S(1)}, f32[1,48,1,64,128]{4,3,2,1,0:T(8,128)}, u32[]{:S(2)}) copy-start(f32[1,48,1,64,128]{4,3,2,1,0:T(8,128)} %select_select_fusion.1) | copy-start | bytes 4718596
  (26 other events, 71.5 us)
Sparse Core Ops, SparseCore 0:
  60.1 32.7 all-gather.6
  94.5 32.6 all-gather.4
  164.6 89.6 all-reduce.1
  316.4 45.5 reduce-scatter.3
where the time goes:
time: 374 us; the launch traced here: 372 us
  waiting for transfers between devices  110 us (29%)
  local copies, waits for them, and re-layouts  81.8 us (22%)
  other arithmetic  75.7 us (20%)
  blocking collectives  74.6 us (20%)
  between operations  15.4 us (4%)
  matrix products  14.1 us (4%)
    psum x1, waiting for transfers between devices, local(): total = lax.psum(term, 'heads')  85.9 us
    unnamed x181, local copies, waits for them, and re-layouts  55.4 us
    psum x2, blocking collectives, token_scale(): return rms_scale(lax.psum(local_sq, 'heads'), inner)  30.6 us
    select_n x2, other arithmetic, recur(): kept = jnp.where((accepted == t + 1)[:, None, None], state, kept)  17.3 us
    all_gather x1, blocking collectives, local(): lax.all_gather(conv_bc_state, 'heads', axis=3, tiled=True)  16.7 us
    unnamed x5, waiting for transfers between devices  16.4 us
    all_gather x1, blocking collectives, local(): lax.all_gather(conv_bc_w, 'heads', axis=2, tiled=True)  15.1 us
    unnamed x14, other arithmetic  12.3 us
  transfers between devices with their start and end apart: 4, of which 3 were waited for; matrix products, arithmetic and copies ran while one was open for 13% of the time, Pallas kernels for 0%

commit v1 on v0

--- a/solution.py
+++ b/solution.py
@@ -50,7 +50,7 @@
 
 
 def token_scale(local_sq, inner):
-    return rms_scale(lax.psum(local_sq, "heads"), inner)
+    return rms_scale(jnp.sum(lax.all_gather(local_sq, "heads"), axis=0), inner)
 
 
 def local(

time: 374 us -> 370 us (0.989)
  blocking collectives: 74.6 us -> 69.7 us
    psum x2 -> x0, blocking collectives: 30.6 us -> none  [token_scale(): return rms_scale(lax.psum(local_sq, 'heads'), inner)]
    all_gather x0 -> x2, blocking collectives: none -> 25.8 us  [token_scale(): return rms_scale(jnp.sum(lax.all_gather(local_sq, 'heads'), axis=0), inner)]
where the time goes in v1:
time: 370 us; the launch traced here: 368 us
  waiting for transfers between devices  111 us (30%)
  local copies, waits for them, and re-layouts  81.8 us (22%)
  other arithmetic  75.8 us (20%)
  blocking collectives  69.7 us (19%)
  between operations  15.3 us (4%)
  matrix products  14.1 us (4%)
    psum x1, waiting for transfers between devices, local(): total = lax.psum(term, 'heads')  86.1 us
    unnamed x181, local copies, waits for them, and re-layouts  56.3 us
    all_gather x2, blocking collectives, token_scale(): return rms_scale(jnp.sum(lax.all_gather(local_sq, 'heads'), axis=0), inner)  25.8 us
    select_n x2, other arithmetic, recur(): kept = jnp.where((accepted == t + 1)[:, None, None], state, kept)  17.2 us
    unnamed x5, waiting for transfers between devices  17 us
    all_gather x1, blocking collectives, local(): lax.all_gather(conv_bc_state, 'heads', axis=3, tiled=True)  16.7 us
    all_gather x1, blocking collectives, local(): lax.all_gather(conv_bc_w, 'heads', axis=2, tiled=True)  15.1 us
    unnamed x14, other arithmetic  12.3 us
  transfers between devices with their start and end apart: 4, of which 3 were waited for; matrix products, arithmetic and copies ran while one was open for 13% of the time, Pallas kernels for 0%

profile of v1, /device:TPU:0, one launch (start us, length us, event | category | flops | bytes accessed | tf_op | source)
XLA Modules:
  0.0 367.9 jit_solution(5121412912445937327)
XLA Ops:
  7.2 43.7 %copy.113 = bf16[50280,320]{1,0:T(8,128)(2,1)} copy(bf16[50280,320]{0,1:T(8,128)(2,1)} %param.21) | data formatting | bytes 64358400 | tf_op args[2]
  51.2 7.8 %gather_fusion = bf16[384,320]{1,0:T(8,128)(2,1)S(1)} fusion(bf16[50280,320]{1,0:T(8,128)(2,1)} %copy.113, s32[1024]{0:T(1024)S(1)} %pad_clamp_fusion), kind=kCustom, calls=%fused_computation | custom fusion | bytes 493056 | tf_op jit(solution)/shard_map/gather | solution.py:147
  59.1 0.9 copy.114
  60.1 0.7 all-gather.7.cloned.1.call-update
  60.8 16.7 %all_gather.22 = bf16[2,48,3,256]{1,3,2,0:T(8,128)(2,1)S(1)} all-gather(bf16[2,48,3,32]{1,3,2,0:T(8,128)(2,1)S(1)} %copy-done.48), channel_id=1, replica_groups=mesh['batch'=4,'heads'=8] {'heads'}, dimensions={3}, use_global_device_ids=true | all-gather | bytes 165888 | tf_op jit(solution)/shard_map/all_gather | solution.py:91
  77.9 15.1 %all_gather.24 = bf16[2,4,256]{1,0,2:T(2,128)(2,1)S(1)} all-gather(bf16[2,4,32]{1,0,2:T(2,128)(2,1)S(1)} %copy.118), channel_id=1, replica_groups=mesh['batch'=4,'heads'=8] {'heads'}, dimensions={2}, use_global_device_ids=true | all-gather | bytes 4608 | tf_op jit(solution)/shard_map/all_gather | solution.py:89
  93.0 12.0 %all-gather.1 = bf16[8,32,2]{1,2,0:T(2,128)(2,1)S(1)} all-gather(bf16[1,32,2]{1,2,0:T(2,128)(2,1)S(1)} %bitcast.580), channel_id=1, replica_groups=mesh['batch'=4,'heads'=8] {'heads'}, dimensions={0}, use_global_device_ids=true | all-gather | bytes 1152 | tf_op jit(solution)/shard_map/all_gather | solution.py:90
  107.1 2.9 slice_reduce_fusion.7
  111.3 2.7 copy.115
  114.5 0.8 copy-done.82
  115.3 0.7 convolution_convert_fusion.1
  116.6 0.7 convolution_reduce_fusion.1
  118.0 0.7 multiply_exponential_fusion.1
  119.7 7.5 %all-gather.7.cloned.1.call-done = bf16[2,2560,256]{1,2,0:T(8,128)(2,1)} async-done(((bf16[2,2560,32]{1,2,0:T(8,128)(2,1)}), bf16[2,2560,256]{1,2,0:T(8,128)(2,1)}) %all-gather.7.cloned.1.call-update) | async-done | bytes 2621456 | tf_op jit(solution)/shard_map/all_gather | solution.py:88
  127.2 2.0 fusion.15
  130.1 1.1 copy-done
  131.2 4.1 %multiply_add_fusion.8 = (f32[1,48,64,128]{3,2,1,0:T(8,128)S(1)}, f32[1,48,64,128]{3,2,1,0:T(8,128)S(1)}, f32[48,64]{1,0:T(8,128)S(1)}, f32[48,64]{1,0:T(8,128)S(1)}) fusion(f32[48,128]{1,0:T(8,128)S(1)} %bitcast.537, f32[48,64]{1,0:T(8,128)S(1)} %get-tuple-element.186, f32[48]{0:T(128)S(1)} %get-tuple-element.237, f32[48,128]{1,0:T(8,128)S(1)} %bitcast.525, ...), kind=kLoop, calls=%fused_computation.43 | loop fusion | flops 7464960 | bytes 4977600 | tf_op jit(solution)/shard_map/vmap()/add | solution.py:37
  136.0 1.6 multiply_reduce_fusion.12
  139.5 3.7 %multiply_reduce_fusion.8 = (f32[48,64]{1,0:T(8,128)S(1)}, f32[48,64]{1,0:T(8,128)S(1)}, f32[48,64]{1,0:T(8,128)S(1)}, f32[48,64]{1,0:T(8,128)S(1)}) fusion(f32[1,48,64,128]{3,2,1,0:T(8,128)S(1)} %get-tuple-element.86, f32[48,128]{1,0:T(8,128)S(1)} %bitcast.566, f32[48,128]{1,0:T(8,128)S(1)} %bitcast.535, f32[48,64]{1,0:T(8,128)S(1)} %get-tuple-element.184, ...), kind=kLoop, calls=%fused_computation.37 | loop fusion | flops 6672384 | bytes 1831488 | tf_op jit(solution)/shard_map/vmap()/reduce_sum | solution.py:40
  145.9 12.8 %all-gather.2 = f32[8,1,384]{2,1,0:T(1,128)S(1)} all-gather(f32[1,1,384]{2,1,0:T(1,128)S(1)} %reshape.2536), channel_id=1, replica_groups=mesh['batch'=4,'heads'=8] {'heads'}, dimensions={0}, use_global_device_ids=true | all-gather | bytes 13824 | tf_op jit(solution)/shard_map/all_gather | solution.py:53
  158.8 3.5 convolution_multiply_fusion.1
  162.6 0.8 copy.125
  163.4 2.9 slice_reduce_fusion.3
  166.3 86.1 %all-reduce.2.cloned.1.call-done = f32[384,2560]{1,0:T(8,128)} async-done(((f32[384,2560]{1,0:T(8,128)}), f32[384,2560]{1,0:T(8,128)}) %all-reduce.2.cloned.1.call-update) | async-done | bytes 3932176 | tf_op jit(solution)/shard_map/psum | solution.py:158
  252.4 2.9 fusion.1
  255.4 0.7 convolution_convert_fusion
  256.6 0.7 convolution_reduce_fusion
  257.5 1.0 fusion.121
  259.2 0.8 fusion.128
  259.9 0.8 fusion.129
  262.7 2.1 fusion.14
  265.6 1.0 bitcast_multiply_fusion.2
  266.9 4.1 %multiply_add_fusion.2 = (f32[1,48,64,128]{3,2,1,0:T(8,128)S(1)}, f32[1,48,64,128]{3,2,1,0:T(8,128)S(1)}, f32[48,64]{1,0:T(8,128)S(1)}, f32[48,64]{1,0:T(8,128)S(1)}) fusion(f32[48,128]{1,0:T(8,128)S(1)} %bitcast.551, f32[48,64]{1,0:T(8,128)S(1)} %get-tuple-element.160, f32[48]{0:T(128)S(1)} %get-tuple-element.51, f32[48,128]{1,0:T(8,128)S(1)} %bitcast.528, ...), kind=kLoop, calls=%fused_computation.29 | loop fusion | flops 7464960 | bytes 4977600 | tf_op jit(solution)/shard_map/vmap()/add | solution.py:37
  271.1 1.2 constant_dynamic-update-slice_fusion.23
  272.3 1.6 multiply_reduce_fusion.4
  273.9 1.2 constant_dynamic-update-slice_fusion.22
  275.1 1.2 constant_dynamic-update-slice_fusion.21
  276.3 1.2 constant_dynamic-update-slice_fusion.20
  277.6 3.7 %multiply_reduce_fusion = (f32[48,64]{1,0:T(8,128)S(1)}, f32[48,64]{1,0:T(8,128)S(1)}, f32[48,64]{1,0:T(8,128)S(1)}, f32[48,64]{1,0:T(8,128)S(1)}) fusion(f32[1,48,64,128]{3,2,1,0:T(8,128)S(1)} %get-tuple-element.82, f32[48,128]{1,0:T(8,128)S(1)} %bitcast.562, f32[48,128]{1,0:T(8,128)S(1)} %bitcast.549, f32[48,64]{1,0:T(8,128)S(1)} %bitcast_multiply_fusion.2, ...), kind=kLoop, calls=%fused_computation.23 | loop fusion | flops 6672384 | bytes 1831488 | tf_op jit(solution)/shard_map/vmap()/reduce_sum | solution.py:40
  281.3 1.2 constant_dynamic-update-slice_fusion.19
  282.5 1.2 constant_dynamic-update-slice_fusion.18
  283.6 1.2 constant_dynamic-update-slice_fusion.17
  284.8 1.9 constant_dynamic-update-slice_fusion.16
  286.9 0.7 copy.135
  287.6 0.8 reshape.2538
  288.4 13.1 %all-gather.3 = f32[8,1,384]{2,1,0:T(1,128)S(1)} all-gather(f32[1,1,384]{2,1,0:T(1,128)S(1)} %reshape.2538), channel_id=1, replica_groups=mesh['batch'=4,'heads'=8] {'heads'}, dimensions={0}, use_global_device_ids=true | all-gather | bytes 13824 | tf_op jit(solution)/shard_map/all_gather | solution.py:53
  301.5 1.1 fusion.71
  302.6 3.5 fusion
  306.1 5.6 %copy.139 = f32[2560,384]{1,0:T(8,128)} copy(f32[2560,384]{0,1:T(8,128)} %fusion) | data formatting | bytes 7864320
  311.7 1.2 broadcast_compare_fusion.7
  313.0 1.7 fusion.105
  314.6 1.4 fusion.119
  316.1 0.7 dynamic-slice_select_fusion.6
  316.8 0.7 copy.136
  317.5 9.0 %select_select_fusion.1 = f32[1,48,1,64,128]{4,3,2,1,0:T(8,128)} fusion(f32[2,48,1,64,128]{4,3,2,1,0:T(8,128)S(1)} %copy-done.1, f32[48,128]{1,0:T(8,128)} %bitcast.536, f32[48,64]{1,0:T(8,128)} %copy-done.34, f32[48,128]{1,0:T(8,128)} %bitcast.534, f32[48,64]{1,0:T(8,128)} %copy-done.35, f32[48,128]{1,0:T(8,128)} %bitcast.532, f32[48,64]{1,0:T(8,128)} %copy-done.33, ...), kind=kLoop, calls=%fused_computation.22 | loop fusion | flops 12582912 | bytes 3442560 | tf_op jit(solution)/shard_map/vmap(jit(_where))/select_n | solution.py:41
  327.9 1.4 pad_maximum_fusion.6
  329.3 0.9 fusion.106
  330.2 1.4 pad_maximum_fusion.5
  331.6 8.2 %select_select_fusion = f32[1,48,1,64,128]{4,3,2,1,0:T(8,128)S(1)} fusion(f32[2,48,1,64,128]{4,3,2,1,0:T(8,128)S(1)} %copy-done.1, f32[48,128]{1,0:T(8,128)} %bitcast.550, f32[48,64]{1,0:T(8,128)} %copy-done.40, f32[48,128]{1,0:T(8,128)} %bitcast.548, f32[48,64]{1,0:T(8,128)} %copy-done.42, f32[48,128]{1,0:T(8,128)} %bitcast.546, f32[48,64]{1,0:T(8,128)} %copy-done.41, ...), kind=kLoop, calls=%fused_computation.21 | loop fusion | flops 12582912 | bytes 3442560 | tf_op jit(solution)/shard_map/vmap(jit(_where))/select_n | solution.py:41
  339.9 1.9 pad_maximum_fusion
  341.8 16.3 %reduce-scatter.4.cloned.1.call-done = f32[320,384]{1,0:T(8,128)} async-done(((f32[2560,384]{1,0:T(8,128)}), f32[320,384]{1,0:T(8,128)}) %reduce-scatter.4.cloned.1.call-update) | async-done | bytes 491536
  358.0 1.3 copy.140
  359.3 1.2 fusion.20
  360.5 0.9 copy.138
  (243 shorter events, 18.1 us)
Async XLA Ops:
  7.2 43.8 %copy-start.73 = (s32[48,8]{0,1:T(8,128)S(1)}, s32[48,8]{0,1:T(8,128)}, u32[]{:S(2)}) copy-start(s32[48,8]{0,1:T(8,128)} %param.19) | copy-start | bytes 4612
  7.2 104.1 %all-gather.9.cloned.1.call-start = ((), (), s32[]{:S(2)}) async-start(), calls=%async_computation.3 | async-start | bytes 2211840 | tf_op jit(solution)/shard_map/all_gather | solution.py:148
  51.2 9.7 %copy-start.48 = (bf16[2,48,3,32]{1,3,2,0:T(8,128)(2,1)S(1)}, bf16[2,48,3,32]{1,3,2,0:T(8,128)(2,1)}, u32[]{:S(2)}) copy-start(bf16[2,48,3,32]{1,3,2,0:T(8,128)(2,1)} %param.37) | copy-start | bytes 55300
  59.0 18.7 %copy-start.74 = (bf16[2,4,32]{2,1,0:T(4,128)(2,1)S(1)}, bf16[2,4,32]{2,1,0:T(4,128)(2,1)}, u32[]{:S(2)}) copy-start(bf16[2,4,32]{2,1,0:T(4,128)(2,1)} %param.31) | copy-start | bytes 1540
  59.0 34.0 %copy-start.81 = (bf16[2,32]{1,0:T(2,128)(2,1)S(1)}, bf16[2,32]{1,0:T(2,128)(2,1)}, u32[]{:S(2)}) copy-start(bf16[2,32]{1,0:T(2,128)(2,1)} %param.32) | copy-start | bytes 388
  59.0 46.1 %copy-start.76 = (f32[2,1]{0,1:T(1,128)S(1)}, f32[2,1]{0,1:T(1,128)}, u32[]{:S(2)}) copy-start(f32[2,1]{0,1:T(1,128)} %param.26) | copy-start | bytes 28
  59.0 46.7 %copy-start.77 = (f32[2,1]{0,1:T(1,128)S(1)}, f32[2,1]{0,1:T(1,128)}, u32[]{:S(2)}) copy-start(f32[2,1]{0,1:T(1,128)} %param.27) | copy-start | bytes 28
  59.1 47.3 %copy-start.78 = (f32[2,1]{0,1:T(1,128)S(1)}, f32[2,1]{0,1:T(1,128)}, u32[]{:S(2)}) copy-start(f32[2,1]{0,1:T(1,128)} %param.28) | copy-start | bytes 28
  59.1 47.8 %copy-start.55 = (f32[2,2560]{1,0:T(2,128)S(1)}, f32[2,2560]{1,0:T(2,128)}, u32[]{:S(2)}) copy-start(f32[2,2560]{1,0:T(2,128)} %param.22) | copy-start | bytes 61444
  60.0 50.1 %copy-start.79 = (bf16[2,64]{1,0:T(2,128)(2,1)S(1)}, bf16[2,64]{1,0:T(2,128)(2,1)}, u32[]{:S(2)}) copy-start(bf16[2,64]{1,0:T(2,128)(2,1)} %param.30) | copy-start | bytes 772
  60.0 50.1 %copy-start.80 = (f32[2,64]{1,0:T(2,128)S(1)}, f32[2,64]{1,0:T(2,128)}, u32[]{:S(2)}) copy-start(f32[2,64]{1,0:T(2,128)} %param.33) | copy-start | bytes 1540
  60.0 51.2 %copy-start.75 = (bf16[2,4,64]{2,1,0:T(4,128)(2,1)S(1)}, bf16[2,4,64]{2,1,0:T(4,128)(2,1)}, u32[]{:S(2)}) copy-start(bf16[2,4,64]{2,1,0:T(4,128)(2,1)} %param.29) | copy-start | bytes 3076
  60.0 51.2 %copy-start.47 = (bf16[2,48,3,64]{3,1,2,0:T(8,128)(2,1)S(1)}, bf16[2,48,3,64]{3,1,2,0:T(8,128)(2,1)}, u32[]{:S(2)}) copy-start(bf16[2,48,3,64]{3,1,2,0:T(8,128)(2,1)} %param.36) | copy-start | bytes 110596
  60.0 67.2 %all-gather.7.cloned.1.call-start = ((), (), s32[]{:S(2)}) async-start(), calls=%async_computation.1 | async-start | bytes 2949120 | tf_op jit(solution)/shard_map/all_gather | solution.py:88
  60.8 191.6 %all-reduce.2.cloned.1.call-start = ((), (), s32[]{:S(2)}) async-start(), calls=%async_computation.2 | async-start | bytes 7864320 | tf_op jit(solution)/shard_map/psum | solution.py:158
  77.8 51.5 %copy-start.10 = (bf16[48,3,256]{2,1,0:T(4,128)(2,1)}, bf16[48,3,256]{2,1,0:T(4,128)(2,1)S(1)}, u32[]{:S(2)}) copy-start(bf16[48,3,256]{2,1,0:T(4,128)(2,1)S(1)} %copy.117) | copy-start | bytes 221188
  111.2 8.1 %copy-start.18 = (bf16[48,3,64]{2,0,1:T(8,128)(2,1)}, bf16[48,3,64]{2,0,1:T(8,128)(2,1)S(1)}, u32[]{:S(2)}) copy-start(bf16[48,3,64]{2,0,1:T(8,128)(2,1)S(1)} %get-tuple-element.194) | copy-start | bytes 55300
  111.3 147.2 %copy-start.17 = (bf16[48,3,64]{2,0,1:T(8,128)(2,1)}, bf16[48,3,64]{2,0,1:T(8,128)(2,1)S(1)}, u32[]{:S(2)}) copy-start(bf16[48,3,64]{2,0,1:T(8,128)(2,1)S(1)} %get-tuple-element.193) | copy-start | bytes 55300
  119.2 10.8 %copy-start.58 = (f32[48]{0:T(128)}, f32[48]{0:T(128)S(1)}, u32[]{:S(2)}) copy-start(f32[48]{0:T(128)S(1)} %get-tuple-element.233) | copy-start | bytes 580
  119.2 10.8 %copy-start.59 = (f32[48]{0:T(128)}, f32[48]{0:T(128)S(1)}, u32[]{:S(2)}) copy-start(f32[48]{0:T(128)S(1)} %get-tuple-element.234) | copy-start | bytes 580
  119.2 10.8 %copy-start.60 = (f32[48]{0:T(128)}, f32[48]{0:T(128)S(1)}, u32[]{:S(2)}) copy-start(f32[48]{0:T(128)S(1)} %get-tuple-element.235) | copy-start | bytes 580
  119.3 10.8 %copy-start.61 = (f32[48]{0:T(128)}, f32[48]{0:T(128)S(1)}, u32[]{:S(2)}) copy-start(f32[48]{0:T(128)S(1)} %get-tuple-element.237) | copy-start | bytes 580
  119.3 16.7 %copy-start.56 = (f32[48]{0:T(128)}, f32[48]{0:T(128)S(1)}, u32[]{:S(2)}) copy-start(f32[48]{0:T(128)S(1)} %get-tuple-element.236) | copy-start | bytes 580
  119.3 20.1 %copy-start.66 = (f32[48]{0:T(128)}, f32[48]{0:T(128)S(1)}, u32[]{:S(2)}) copy-start(f32[48]{0:T(128)S(1)} %get-tuple-element.238) | copy-start | bytes 580
  119.3 20.1 %copy-start.67 = (f32[48]{0:T(128)}, f32[48]{0:T(128)S(1)}, u32[]{:S(2)}) copy-start(f32[48]{0:T(128)S(1)} %get-tuple-element.239) | copy-start | bytes 580
  119.3 20.1 %copy-start.68 = (f32[48]{0:T(128)}, f32[48]{0:T(128)S(1)}, u32[]{:S(2)}) copy-start(f32[48]{0:T(128)S(1)} %get-tuple-element.240) | copy-start | bytes 580
  119.6 10.5 %copy-start.36 = (f32[48,64]{1,0:T(8,128)}, f32[48,64]{1,0:T(8,128)S(1)}, u32[]{:S(2)}) copy-start(f32[48,64]{1,0:T(8,128)S(1)} %get-tuple-element.186) | copy-start | bytes 36868
  119.6 10.5 %copy-start.37 = (f32[48,64]{1,0:T(8,128)}, f32[48,64]{1,0:T(8,128)S(1)}, u32[]{:S(2)}) copy-start(f32[48,64]{1,0:T(8,128)S(1)} %get-tuple-element.188) | copy-start | bytes 36868
  119.6 10.5 %copy-start.38 = (f32[48,64]{1,0:T(8,128)}, f32[48,64]{1,0:T(8,128)S(1)}, u32[]{:S(2)}) copy-start(f32[48,64]{1,0:T(8,128)S(1)} %get-tuple-element.189) | copy-start | bytes 36868
  119.6 10.5 %copy-start.39 = (f32[48,64]{1,0:T(8,128)}, f32[48,64]{1,0:T(8,128)S(1)}, u32[]{:S(2)}) copy-start(f32[48,64]{1,0:T(8,128)S(1)} %get-tuple-element.190) | copy-start | bytes 36868
  119.6 16.3 %copy-start.15 = (f32[48,64]{1,0:T(8,128)}, f32[48,64]{1,0:T(8,128)S(1)}, u32[]{:S(2)}) copy-start(f32[48,64]{1,0:T(8,128)S(1)} %get-tuple-element.187) | copy-start | bytes 36868
  119.7 19.8 %copy-start.33 = (f32[48,64]{1,0:T(8,128)}, f32[48,64]{1,0:T(8,128)S(1)}, u32[]{:S(2)}) copy-start(f32[48,64]{1,0:T(8,128)S(1)} %get-tuple-element.183) | copy-start | bytes 36868
  119.7 19.8 %copy-start.34 = (f32[48,64]{1,0:T(8,128)}, f32[48,64]{1,0:T(8,128)S(1)}, u32[]{:S(2)}) copy-start(f32[48,64]{1,0:T(8,128)S(1)} %get-tuple-element.184) | copy-start | bytes 36868
  119.7 19.8 %copy-start.35 = (f32[48,64]{1,0:T(8,128)}, f32[48,64]{1,0:T(8,128)S(1)}, u32[]{:S(2)}) copy-start(f32[48,64]{1,0:T(8,128)S(1)} %get-tuple-element.185) | copy-start | bytes 36868
  130.0 5.4 %copy-start.22 = (f32[48,1,128]{2,1,0:T(1,128)}, f32[48,1,128]{2,1,0:T(1,128)S(1)}, u32[]{:S(2)}) copy-start(f32[48,1,128]{2,1,0:T(1,128)S(1)} %get-tuple-element.174) | copy-start | bytes 73732
  130.0 5.4 %copy-start.23 = (f32[48,1,128]{2,1,0:T(1,128)}, f32[48,1,128]{2,1,0:T(1,128)S(1)}, u32[]{:S(2)}) copy-start(f32[48,1,128]{2,1,0:T(1,128)S(1)} %get-tuple-element.178) | copy-start | bytes 73732
  130.0 5.4 %copy-start.24 = (f32[48,1,128]{2,1,0:T(1,128)}, f32[48,1,128]{2,1,0:T(1,128)S(1)}, u32[]{:S(2)}) copy-start(f32[48,1,128]{2,1,0:T(1,128)S(1)} %get-tuple-element.180) | copy-start | bytes 73732
  130.0 5.4 %copy-start.25 = (f32[48,1,128]{2,1,0:T(1,128)}, f32[48,1,128]{2,1,0:T(1,128)S(1)}, u32[]{:S(2)}) copy-start(f32[48,1,128]{2,1,0:T(1,128)S(1)} %get-tuple-element.181) | copy-start | bytes 73732
  130.0 6.0 %copy-start.13 = (f32[48,1,128]{2,1,0:T(1,128)}, f32[48,1,128]{2,1,0:T(1,128)S(1)}, u32[]{:S(2)}) copy-start(f32[48,1,128]{2,1,0:T(1,128)S(1)} %get-tuple-element.176) | copy-start | bytes 73732
  130.0 9.5 %copy-start.19 = (f32[48,1,128]{2,1,0:T(1,128)}, f32[48,1,128]{2,1,0:T(1,128)S(1)}, u32[]{:S(2)}) copy-start(f32[48,1,128]{2,1,0:T(1,128)S(1)} %get-tuple-element.170) | copy-start | bytes 73732
  130.0 9.5 %copy-start.20 = (f32[48,1,128]{2,1,0:T(1,128)}, f32[48,1,128]{2,1,0:T(1,128)S(1)}, u32[]{:S(2)}) copy-start(f32[48,1,128]{2,1,0:T(1,128)S(1)} %get-tuple-element.171) | copy-start | bytes 73732
  130.0 9.5 %copy-start.21 = (f32[48,1,128]{2,1,0:T(1,128)}, f32[48,1,128]{2,1,0:T(1,128)S(1)}, u32[]{:S(2)}) copy-start(f32[48,1,128]{2,1,0:T(1,128)S(1)} %get-tuple-element.172) | copy-start | bytes 73732
  162.3 195.7 %reduce-scatter.4.cloned.1.call-start = ((), (), s32[]{:S(2)}) async-start(), calls=%async_computation.4 | async-start | bytes 4423680
  262.7 9.6 %copy-start.57 = (f32[48]{0:T(128)}, f32[48]{0:T(128)S(1)}, u32[]{:S(2)}) copy-start(f32[48]{0:T(128)S(1)} %get-tuple-element.52) | copy-start | bytes 580
  262.7 14.8 %copy-start.69 = (f32[48]{0:T(128)}, f32[48]{0:T(128)S(1)}, u32[]{:S(2)}) copy-start(f32[48]{0:T(128)S(1)} %get-tuple-element.48) | copy-start | bytes 580
  262.7 14.8 %copy-start.70 = (f32[48]{0:T(128)}, f32[48]{0:T(128)S(1)}, u32[]{:S(2)}) copy-start(f32[48]{0:T(128)S(1)} %get-tuple-element.49) | copy-start | bytes 580
  262.7 14.8 %copy-start.71 = (f32[48]{0:T(128)}, f32[48]{0:T(128)S(1)}, u32[]{:S(2)}) copy-start(f32[48]{0:T(128)S(1)} %get-tuple-element.50) | copy-start | bytes 580
  265.5 5.5 %copy-start.29 = (f32[48,1,128]{2,1,0:T(1,128)}, f32[48,1,128]{2,1,0:T(1,128)S(1)}, u32[]{:S(2)}) copy-start(f32[48,1,128]{2,1,0:T(1,128)S(1)} %get-tuple-element.149) | copy-start | bytes 73732
  265.6 5.5 %copy-start.30 = (f32[48,1,128]{2,1,0:T(1,128)}, f32[48,1,128]{2,1,0:T(1,128)S(1)}, u32[]{:S(2)}) copy-start(f32[48,1,128]{2,1,0:T(1,128)S(1)} %get-tuple-element.153) | copy-start | bytes 73732
  265.6 5.5 %copy-start.31 = (f32[48,1,128]{2,1,0:T(1,128)}, f32[48,1,128]{2,1,0:T(1,128)S(1)}, u32[]{:S(2)}) copy-start(f32[48,1,128]{2,1,0:T(1,128)S(1)} %get-tuple-element.155) | copy-start | bytes 73732
  265.6 5.5 %copy-start.32 = (f32[48,1,128]{2,1,0:T(1,128)}, f32[48,1,128]{2,1,0:T(1,128)S(1)}, u32[]{:S(2)}) copy-start(f32[48,1,128]{2,1,0:T(1,128)S(1)} %get-tuple-element.156) | copy-start | bytes 73732
  265.6 6.7 %copy-start.14 = (f32[48,1,128]{2,1,0:T(1,128)}, f32[48,1,128]{2,1,0:T(1,128)S(1)}, u32[]{:S(2)}) copy-start(f32[48,1,128]{2,1,0:T(1,128)S(1)} %get-tuple-element.151) | copy-start | bytes 73732
  265.6 11.9 %copy-start.26 = (f32[48,1,128]{2,1,0:T(1,128)}, f32[48,1,128]{2,1,0:T(1,128)S(1)}, u32[]{:S(2)}) copy-start(f32[48,1,128]{2,1,0:T(1,128)S(1)} %get-tuple-element.145) | copy-start | bytes 73732
  265.6 11.9 %copy-start.27 = (f32[48,1,128]{2,1,0:T(1,128)}, f32[48,1,128]{2,1,0:T(1,128)S(1)}, u32[]{:S(2)}) copy-start(f32[48,1,128]{2,1,0:T(1,128)S(1)} %get-tuple-element.146) | copy-start | bytes 73732
  265.6 11.9 %copy-start.28 = (f32[48,1,128]{2,1,0:T(1,128)}, f32[48,1,128]{2,1,0:T(1,128)S(1)}, u32[]{:S(2)}) copy-start(f32[48,1,128]{2,1,0:T(1,128)S(1)} %get-tuple-element.147) | copy-start | bytes 73732
  266.6 10.9 %copy-start.40 = (f32[48,64]{1,0:T(8,128)}, f32[48,64]{1,0:T(8,128)S(1)}, u32[]{:S(2)}) copy-start(f32[48,64]{1,0:T(8,128)S(1)} %bitcast_multiply_fusion.2) | copy-start | bytes 36868
  266.8 4.3 %copy-start.43 = (f32[48,64]{1,0:T(8,128)}, f32[48,64]{1,0:T(8,128)S(1)}, u32[]{:S(2)}) copy-start(f32[48,64]{1,0:T(8,128)S(1)} %get-tuple-element.160) | copy-start | bytes 36868
  266.8 5.5 %copy-start.16 = (f32[48,64]{1,0:T(8,128)}, f32[48,64]{1,0:T(8,128)S(1)}, u32[]{:S(2)}) copy-start(f32[48,64]{1,0:T(8,128)S(1)} %get-tuple-element.161) | copy-start | bytes 36868
  266.8 10.7 %copy-start.41 = (f32[48,64]{1,0:T(8,128)}, f32[48,64]{1,0:T(8,128)S(1)}, u32[]{:S(2)}) copy-start(f32[48,64]{1,0:T(8,128)S(1)} %get-tuple-element.158) | copy-start | bytes 36868
  266.8 10.7 %copy-start.42 = (f32[48,64]{1,0:T(8,128)}, f32[48,64]{1,0:T(8,128)S(1)}, u32[]{:S(2)}) copy-start(f32[48,64]{1,0:T(8,128)S(1)} %get-tuple-element.159) | copy-start | bytes 36868
  273.9 12.8 %copy-start.8 = (bf16[48,8,1,1,64]{4,3,1,0,2:T(2,128)(2,1)S(1)}, bf16[48,8,1,1,64]{4,3,1,0,2:T(2,128)(2,1)}, u32[]{:S(2)}) copy-start(bf16[48,8,1,1,64]{4,3,1,0,2:T(2,128)(2,1)} %get-tuple-element.140) | copy-start | bytes 147460
  317.5 9.0 %copy-start.12 = (bf16[48,3,256]{2,1,0:T(4,128)(2,1)S(1)}, bf16[48,3,256]{2,1,0:T(4,128)(2,1)}, u32[]{:S(2)}) copy-start(bf16[48,3,256]{2,1,0:T(4,128)(2,1)} %copy.125) | copy-start | bytes 221188
  317.5 9.0 %copy-start.54 = (pred[48]{0:T(512)(128)(4,1)S(1)}, pred[48]{0:T(512)(128)(4,1)}, u32[]{:S(2)}) copy-start(pred[48]{0:T(512)(128)(4,1)} %copy-done.53) | copy-start | bytes 148
  331.6 8.3 %copy-start.2 = (f32[1,48,1,64,128]{4,3,2,1,0:T(8,128)S(1)}, f32[1,48,1,64,128]{4,3,2,1,0:T(8,128)}, u32[]{:S(2)}) copy-start(f32[1,48,1,64,128]{4,3,2,1,0:T(8,128)} %select_select_fusion.1) | copy-start | bytes 4718596
  (25 other events, 67.2 us)
Sparse Core Ops, SparseCore 0:
  60.1 32.7 all-gather.8
  94.5 32.6 all-gather.6
  162.4 89.9 all-reduce.1
  311.8 46.1 reduce-scatter.3
